TPU v7x, 128 devices: a whole 4x4x4 slice. The times are simulated.
128 devices in a mesh: ka: 16 (over x_hi, z, core), band: 8 (over x_lo, y).
Axes of the slice: x: 4 (x_hi: 2, x_lo: 2; x = x_hi * 2 + x_lo), y: 4, z: 4, core: 2. Of those that a mesh axis runs over, the one named last changes fastest.
Arguments:
- occ_rows: bfloat16 [16, 2048, 128], P('ka', 'band'), may hold values from -0.5 to 0.5
- vir_rows: bfloat16 [16, 2048, 896], P('ka', 'band'), may hold values from -0.1875 to 0.1875
- trial_vectors: float32 [16, 2, 128, 896], P('ka', None, None, 'band'), may hold values from -6 to 6
- occ_energy: float32 [16, 128], P('ka'), may hold values from -1.2 to -0.3
- vir_energy: float32 [16, 896], P('ka', 'band'), may hold values from 0.1 to 1.5
- coulomb: bfloat16 [2048, 2048], P('band'), may hold values from -0.0625 to 0.0625
- exch_kernel: bfloat16 [16, 2048, 2048], P(None, 'band'), as said below
- minus_table: int32 [16, 16], replicated, may hold values from 0 to 15, as said below
Outputs:
- sigma_vectors: float32 [16, 2, 128, 896], P('ka', None, None, 'band')
Inputs may be any that keep to these rules, and one draw needn't show every extreme that they name: minus_table[k, q] is the k-point k - q on a group of 16 k-points: every row and every column holds each index once, and one q gives minus_table[k, q] == k for every k. Each exch_kernel[q] is symmetric.
All inputs are finite; a program needn't handle non-finite values.
Results may differ from a plain program's by a relative error of at most 0.0051.
Values may be sent and summed in bfloat16 or wider, within the bound.
A program may use at most 128 MiB of HBM per device.

v0:
```python
import jax
import jax.numpy as jnp
from jax import lax
from jax.sharding import PartitionSpec as P


def sent_to_all(array, axis):
    copies = jnp.broadcast_to(array, (lax.axis_size(axis), *array.shape))
    return lax.all_to_all(copies, axis, split_axis=0, concat_axis=0, tiled=True)


def taken_together(array, axis):
    return sent_to_all(array, axis).sum(axis=0)


def in_order(pieces, dim):
    pieces = jnp.moveaxis(pieces, 0, dim)
    dims = pieces.shape
    return pieces.reshape(*dims[:dim], dims[dim] * dims[dim + 1], *dims[dim + 2 :])


def gather_directly(array, axis, dim):
    pieces = sent_to_all(array, axis)
    return in_order(pieces, dim)


def split_up(array, dim, size):
    before, after = (array.shape[:dim], array.shape[dim + 1 :])
    return jnp.moveaxis(array.reshape(*before, size, -1, *after), dim, 0)


def summed_on_arrival(array, axis, dim):
    size = lax.axis_size(axis)
    pieces = lax.all_to_all(split_up(array, dim, size), axis, 0, 0, tiled=True)
    return jnp.sum(pieces, axis=0)


def per_device(
    occ_rows, vir_rows, trial_vectors, occ_energy, vir_energy, coulomb, exch_kernel, minus_table
):
    vectors = trial_vectors.shape[1]
    own_rows = occ_rows.shape[1]
    kpoints = lax.axis_size("ka")
    self_point = lax.axis_index("ka")
    trial_half = trial_vectors[0].astype(jnp.bfloat16)
    trial_full, vir_full = (
        lax.all_gather(trial_half, "band", axis=2, tiled=True),
        lax.all_gather(vir_rows[0], "band", axis=0, tiled=True),
    )
    auxiliary = vir_full.shape[0]
    occ_own = occ_rows[0]
    vir_own = vir_rows[0]
    mixed_rows = jnp.einsum(
        "ri,via->vra", occ_own, trial_full, preferred_element_type=jnp.float32
    ).astype(jnp.bfloat16)
    pair_block = jnp.einsum(
        "vra,na->vrn", mixed_rows, vir_full, preferred_element_type=jnp.float32
    ).astype(jnp.bfloat16)
    density_own = jnp.sum(
        mixed_rows.astype(jnp.float32) * vir_own.astype(jnp.float32)[None], axis=2
    )
    density_sum = taken_together(density_own, "ka")
    density_half = gather_directly(density_sum.astype(jnp.bfloat16), "band", 1)
    potential = jnp.einsum("vn,rn->vr", density_half, coulomb, preferred_element_type=jnp.float32)
    piece_width = auxiliary // kpoints
    kernel_cols = lax.dynamic_slice_in_dim(exch_kernel, self_point * piece_width, piece_width, 2)
    split_pairs = pair_block.reshape(vectors, own_rows, kpoints, piece_width)
    moved_pairs = jnp.take(
        lax.all_to_all(split_pairs, "ka", split_axis=2, concat_axis=2, tiled=True),
        minus_table,
        axis=2,
    )
    summed = jnp.einsum(
        "vrkqc,qrc->vrkc", moved_pairs, kernel_cols, preferred_element_type=jnp.float32
    )
    screened = lax.all_to_all(
        summed.astype(jnp.bfloat16), "ka", split_axis=2, concat_axis=2, tiled=True
    )
    screened = screened.reshape(vectors, own_rows, auxiliary)
    product = jnp.einsum("vrn,na->vra", screened, vir_full, preferred_element_type=jnp.float32)
    weights = (2.0 * potential[:, :, None] * vir_own.astype(jnp.float32)[None] - product).astype(
        jnp.bfloat16
    )
    partial_sums = jnp.einsum("ri,vra->via", occ_own, weights, preferred_element_type=jnp.float32)
    coupled = summed_on_arrival(partial_sums, "band", 2)
    energy_gaps = vir_energy[0][None, :] - occ_energy[0][:, None]
    return (energy_gaps[None] * trial_vectors[0] + coupled)[None]


def solution(mesh):
    in_specs = (
        P("ka", "band", None),
        P("ka", "band", None),
        P("ka", None, None, "band"),
        P("ka", None),
        P("ka", "band"),
        P("band", None),
        P(None, "band", None),
        P(),
    )
    out_specs = P("ka", None, None, "band")
    return jax.shard_map(
        per_device, mesh=mesh, in_specs=in_specs, out_specs=out_specs, check_vma=False
    )
```

profile of v0, /device:TPU:96, one launch (start us, length us, event | category | flops | bytes accessed | tf_op | source)
XLA Modules:
  0.0 215.4 jit_solution(1257399889311923718)
XLA Ops:
  6.5 0.0 copy-start
  6.5 0.0 copy-start.3
  6.5 0.0 copy-start.4
  6.5 0.0 all-gather.4.cloned.1.call-start
  6.5 0.7 all-gather.4.cloned.1.call-update
  7.3 1.1 bitcast_convert_fusion.1
  8.3 0.3 copy.30
  8.7 0.0 copy-done.3
  8.7 0.0 copy-start.2
  8.7 31.1 %all-gather = bf16[1,2,128,896]{2,3,1,0:T(8,128)(2,1)S(1)} all-gather(bf16[1,2,128,112]{2,3,1,0:T(8,128)(2,1)S(1)} %convert_element_type.33), channel_id=2, replica_groups=mesh['ka'=16,'band'=8] {'band'}, dimensions={3}, use_global_device_ids=true | all-gather | bytes 516096 | tf_op jit(solution)/shard_map/all_gather | solution.py:47
  39.7 0.0 copy-done.4
  39.7 0.4 multiply_reduce_fusion.1
  40.2 0.6 broadcast_in_dim.23
  40.8 6.5 %all-to-all-start = ((f32[16,2,256]{2,1,0:T(2,128)}), f32[16,2,256]{2,1,0:T(2,128)S(1)}, u32[]{:S(2)}, u32[]{:S(2)}) async-start(f32[16,2,256]{2,1,0:T(2,128)} %broadcast_in_dim.23), calls=%async_computation | async-start | bytes 65536 | tf_op jit(solution)/shard_map/all_to_all | solution.py:9
  47.3 13.7 %all-gather.4.cloned.1.call-done = bf16[1,2048,896]{2,1,0:T(8,128)(2,1)} async-done(((bf16[1,256,896]{2,1,0:T(8,128)(2,1)}), bf16[1,2048,896]{2,1,0:T(8,128)(2,1)}) %all-gather.4.cloned.1.call-update) | async-done | bytes 3670032 | tf_op jit(solution)/shard_map/all_gather | solution.py:48
  61.0 4.4 %fusion.7 = bf16[2,32,16,8,128]{4,3,2,1,0:T(8,128)(2,1)S(1)} fusion(bf16[2,256,896]{1,2,0:T(8,128)(2,1)S(1)} %get-tuple-element.6, bf16[1,2048,896]{2,1,0:T(8,128)(2,1)} %all-gather.4.cloned.1.call-done), kind=kOutput, calls=%fused_computation.11 | convolution fusion | flops 1880096768 | bytes 6684672 | tf_op jit(solution)/shard_map/vra,na->vrn/dot_general | solution.py:56
  65.5 0.0 copy-done.2
  65.5 1.9 copy.55
  67.4 0.0 all-to-all-done
  67.4 0.0 copy-start.5
  67.4 6.8 %all-to-all-start.2 = ((bf16[2,256,16,128]{3,1,0,2:T(8,128)(2,1)}), bf16[2,256,16,128]{3,1,0,2:T(8,128)(2,1)S(1)}, u32[]{:S(2)}, u32[]{:S(2)}) async-start(bf16[2,256,16,128]{3,1,0,2:T(8,128)(2,1)} %bitcast.66), calls=%async_computation.2 | async-start | bytes 4194304 | tf_op jit(solution)/shard_map/all_to_all | solution.py:69
  74.2 0.0 copy-done.5
  74.2 0.1 reshape.57
  74.3 2.7 %bitcast_convert_fusion = f32[256,128,16]{1,0,2:T(8,128)} fusion(bf16[16,256,2048]{2,1,0:T(8,128)(2,1)} %param.14, s32[]{:T(128)S(6)} %select_n.12), kind=kLoop, calls=%fused_computation.16 | loop fusion | flops 524288 | bytes 3145732
  77.0 26.1 %all-to-all-done.2 = bf16[2,256,16,128]{3,1,0,2:T(8,128)(2,1)S(1)} async-done(((bf16[2,256,16,128]{3,1,0,2:T(8,128)(2,1)}), bf16[2,256,16,128]{3,1,0,2:T(8,128)(2,1)S(1)}, u32[]{:S(2)}, u32[]{:S(2)}) %all-to-all-start.2) | async-done | bytes 2097184 | tf_op jit(solution)/shard_map/all_to_all | solution.py:69
  103.1 0.0 copy-start.1
  103.1 0.6 broadcast_in_dim.24
  103.7 0.7 copy-done.1
  104.4 4.2 %all-to-all-start.1 = ((bf16[8,2,256]{2,1,0:T(2,128)(2,1)}), bf16[8,2,256]{2,1,0:T(2,128)(2,1)S(1)}, u32[]{:S(2)}, u32[]{:S(2)}) async-start(bf16[8,2,256]{2,1,0:T(2,128)(2,1)} %broadcast_in_dim.24), calls=%async_computation.1 | async-start | bytes 16384 | tf_op jit(solution)/shard_map/all_to_all | solution.py:9
  108.6 1.7 copy.34
  110.3 13.9 %gather_fusion = bf16[256,2,256,128]{3,2,1,0:T(8,128)(2,1)} fusion(bf16[2,256,16,128]{3,1,2,0:T(8,128)(2,1)S(1)} %copy.34, s32[1024]{0:T(1024)S(1)} %pad_clamp_fusion), kind=kCustom, calls=%fused_computation | custom fusion | bytes 67109888 | tf_op jit(solution)/shard_map/jit(_take)/gather | solution.py:68
  124.2 17.9 %multiply_reduce_fusion = bf16[256,128,2,16]{1,0,2,3:T(8,128)(2,1)S(1)} fusion(f32[256,128,16]{1,0,2:T(8,128)} %bitcast_convert_fusion, bf16[16,16,2,256,128]{4,3,2,1,0:T(8,128)(2,1)} %bitcast.65, pred[16,16]{1,0:T(8,128)(4,1)S(1)} %compare_and_fusion), kind=kLoop, calls=%fused_computation.1 | loop fusion | flops 66060288 | bytes 37748992
  142.1 2.6 %copy.47 = bf16[256,128,2,16]{0,1,2,3:T(8,128)(2,1)} copy(bf16[256,128,2,16]{1,0,2,3:T(8,128)(2,1)S(1)} %multiply_reduce_fusion) | data formatting | bytes 4194304 | tf_op jit(solution)/shard_map/vrkqc,qrc->vrkc/dot_general | solution.py:73
  144.7 0.0 all-to-all-done.1
  144.7 5.5 %all-to-all-start.3 = ((bf16[2,256,16,128]{1,3,0,2:T(8,128)(2,1)}), bf16[2,256,16,128]{1,3,0,2:T(8,128)(2,1)S(1)}, u32[]{:S(2)}, u32[]{:S(2)}) async-start(bf16[2,256,16,128]{1,3,0,2:T(8,128)(2,1)} %bitcast.67), calls=%async_computation.3 | async-start | bytes 4194304 | tf_op jit(solution)/shard_map/all_to_all | solution.py:76
  150.3 0.0 copy-done
  150.3 0.4 convolution_multiply_fusion
  150.6 28.5 %all-to-all-done.3 = bf16[2,256,16,128]{1,3,0,2:T(8,128)(2,1)S(1)} async-done(((bf16[2,256,16,128]{1,3,0,2:T(8,128)(2,1)}), bf16[2,256,16,128]{1,3,0,2:T(8,128)(2,1)S(1)}, u32[]{:S(2)}, u32[]{:S(2)}) %all-to-all-start.3) | async-done | bytes 2097184 | tf_op jit(solution)/shard_map/all_to_all | solution.py:76
  179.2 1.5 copy.35
  180.7 5.6 %fusion.14 = f32[2,896,128]{2,1,0:T(8,128)S(1)} fusion(bf16[2,256,2048]{1,2,0:T(8,128)(2,1)} %bitcast.68, bf16[1,2048,896]{2,1,0:T(8,128)(2,1)} %all-gather.4.cloned.1.call-done, f32[2,256]{1,0:T(2,128)S(1)} %convolution_multiply_fusion, f32[256,896]{0,1:T(8,128)} %copy-done.2, bf16[1,256,128]{2,1,0:T(8,128)(2,1)S(1)} %copy-done.4), kind=kOutput, calls=%fused_computation.14 | convolution fusion | flops 1997864960 | bytes 7669760 | tf_op jit(solution)/shard_map/ri,vra->via/dot_general | solution.py:84
  186.2 0.0 copy-start.6
  186.2 0.0 copy-start.7
  186.3 1.0 copy.56
  187.2 6.6 %all-to-all-start.4 = ((f32[8,2,128,112]{2,3,1,0:T(8,128)}), f32[8,2,128,112]{2,3,1,0:T(8,128)S(1)}, u32[]{:S(2)}, u32[]{:S(2)}) async-start(f32[8,2,128,112]{2,3,1,0:T(8,128)} %bitcast.64), calls=%async_computation.4 | async-start | bytes 1835008 | tf_op jit(solution)/shard_map/all_to_all | solution.py:34
  193.9 0.0 copy-done.6
  193.9 0.0 copy-done.7
  193.9 0.1 broadcast_subtract_fusion
  194.0 13.9 %all-to-all-done.4 = f32[8,2,128,112]{2,3,1,0:T(8,128)S(1)} async-done(((f32[8,2,128,112]{2,3,1,0:T(8,128)}), f32[8,2,128,112]{2,3,1,0:T(8,128)S(1)}, u32[]{:S(2)}, u32[]{:S(2)}) %all-to-all-start.4) | async-done | bytes 917536 | tf_op jit(solution)/shard_map/all_to_all | solution.py:34
  207.9 0.7 bitcast_add_fusion
  (6 shorter events, 0.1 us)
Async XLA Ops:
  6.5 143.7 %copy-start = (bf16[256,2048]{1,0:T(8,128)(2,1)S(1)}, bf16[256,2048]{1,0:T(8,128)(2,1)}, u32[]{:S(2)}) copy-start(bf16[256,2048]{1,0:T(8,128)(2,1)} %param.13) | copy-start | bytes 3145732
  6.5 2.1 copy-start.3
  6.5 33.2 %copy-start.4 = (bf16[1,256,128]{2,1,0:T(8,128)(2,1)S(1)}, bf16[1,256,128]{2,1,0:T(8,128)(2,1)}, u32[]{:S(2)}) copy-start(bf16[1,256,128]{2,1,0:T(8,128)(2,1)} %param.8) | copy-start | bytes 196612
  6.5 54.5 %all-gather.4.cloned.1.call-start = ((), (), s32[]{:S(2)}) async-start(), calls=%async_computation.5 | async-start | bytes 4128768 | tf_op jit(solution)/shard_map/all_gather | solution.py:48
  8.7 56.8 %copy-start.2 = (f32[256,896]{0,1:T(8,128)}, f32[256,896]{0,1:T(8,128)S(1)}, u32[]{:S(2)}) copy-start(f32[256,896]{0,1:T(8,128)S(1)} %copy.30) | copy-start | bytes 2752516
  40.8 26.6 %all-to-all-start = ((f32[16,2,256]{2,1,0:T(2,128)}), f32[16,2,256]{2,1,0:T(2,128)S(1)}, u32[]{:S(2)}, u32[]{:S(2)}) async-start(f32[16,2,256]{2,1,0:T(2,128)} %broadcast_in_dim.23), calls=%async_computation | async-start | bytes 65536 | tf_op jit(solution)/shard_map/all_to_all | solution.py:9
  67.4 6.8 %copy-start.5 = (s32[16,16]{1,0:T(8,128)S(1)}, s32[16,16]{1,0:T(8,128)}, u32[]{:S(2)}) copy-start(s32[16,16]{1,0:T(8,128)} %param.15) | copy-start | bytes 3076
  67.4 35.7 %all-to-all-start.2 = ((bf16[2,256,16,128]{3,1,0,2:T(8,128)(2,1)}), bf16[2,256,16,128]{3,1,0,2:T(8,128)(2,1)S(1)}, u32[]{:S(2)}, u32[]{:S(2)}) async-start(bf16[2,256,16,128]{3,1,0,2:T(8,128)(2,1)} %bitcast.66), calls=%async_computation.2 | async-start | bytes 4194304 | tf_op jit(solution)/shard_map/all_to_all | solution.py:69
  103.1 1.3 copy-start.1
  104.4 40.3 %all-to-all-start.1 = ((bf16[8,2,256]{2,1,0:T(2,128)(2,1)}), bf16[8,2,256]{2,1,0:T(2,128)(2,1)S(1)}, u32[]{:S(2)}, u32[]{:S(2)}) async-start(bf16[8,2,256]{2,1,0:T(2,128)(2,1)} %broadcast_in_dim.24), calls=%async_computation.1 | async-start | bytes 16384 | tf_op jit(solution)/shard_map/all_to_all | solution.py:9
  144.7 34.5 %all-to-all-start.3 = ((bf16[2,256,16,128]{1,3,0,2:T(8,128)(2,1)}), bf16[2,256,16,128]{1,3,0,2:T(8,128)(2,1)S(1)}, u32[]{:S(2)}, u32[]{:S(2)}) async-start(bf16[2,256,16,128]{1,3,0,2:T(8,128)(2,1)} %bitcast.67), calls=%async_computation.3 | async-start | bytes 4194304 | tf_op jit(solution)/shard_map/all_to_all | solution.py:76
  186.2 7.6 %copy-start.6 = (f32[1,128]{1,0:T(1,128)S(1)}, f32[1,128]{1,0:T(1,128)}, u32[]{:S(2)}) copy-start(f32[1,128]{1,0:T(1,128)} %param.11) | copy-start | bytes 1540
  186.2 7.6 %copy-start.7 = (f32[1,112]{1,0:T(1,128)S(1)}, f32[1,112]{1,0:T(1,128)}, u32[]{:S(2)}) copy-start(f32[1,112]{1,0:T(1,128)} %param.12) | copy-start | bytes 1348
  187.2 20.6 %all-to-all-start.4 = ((f32[8,2,128,112]{2,3,1,0:T(8,128)}), f32[8,2,128,112]{2,3,1,0:T(8,128)S(1)}, u32[]{:S(2)}, u32[]{:S(2)}) async-start(f32[8,2,128,112]{2,3,1,0:T(8,128)} %bitcast.64), calls=%async_computation.4 | async-start | bytes 1835008 | tf_op jit(solution)/shard_map/all_to_all | solution.py:34
Sparse Core Ops, SparseCore 0:
  9.0 52.0 all-gather.3
where the time goes:
time: 216 us; the launch traced here: 215 us
  waiting for transfers between devices  82.9 us (38%)
  blocking collectives  31.1 us (14%)
  starting transfers between devices  29.6 us (14%)
  local copies, waits for them, and re-layouts  25 us (12%)
  other arithmetic  22.5 us (10%)
  between operations  13.5 us (6%)
  matrix products  10.8 us (5%)
    all_gather x1, blocking collectives, per_device(): lax.all_gather(trial_half, 'band', axis=2, tiled=True)  31.1 us
    all_to_all x1, waiting for transfers between devices, per_device(): lax.all_to_all(summed.astype(jnp.bfloat16), 'ka', split_axis=2, concat_ax...  28.5 us
    all_to_all x1, waiting for transfers between devices, per_device(): lax.all_to_all(split_pairs, 'ka', split_axis=2, concat_axis=2, tiled=True)  26.1 us
    unnamed x2, other arithmetic  20.6 us
    gather x1, local copies, waits for them, and re-layouts, per_device(): jnp.take(lax.all_to_all(split_pairs, 'ka', split_axis=2, concat_axis=2, t...  13.9 us
    all_to_all x1, waiting for transfers between devices, summed_on_arrival(): pieces = lax.all_to_all(split_up(array, dim, size), axis, 0, 0, tiled=True)  13.9 us
    all_gather x1, waiting for transfers between devices, per_device(): lax.all_gather(vir_rows[0], 'band', axis=0, tiled=True)  13.7 us
    all_to_all x2, starting transfers between devices, sent_to_all(): return lax.all_to_all(copies, axis, split_axis=0, concat_axis=0, tiled=True)  10.7 us
  transfers between devices with their start and end apart: 6, of which 4 were waited for; matrix products, arithmetic and copies ran while one was open for 22% of the time, Pallas kernels for 0%

commit v1 on v0

--- a/solution.py
+++ b/solution.py
@@ -45,7 +45,9 @@
     trial_half = trial_vectors[0].astype(jnp.bfloat16)
     trial_full, vir_full = (
         lax.all_gather(trial_half, "band", axis=2, tiled=True),
-        lax.all_gather(vir_rows[0], "band", axis=0, tiled=True),
+        jnp.concatenate(
+            lax.all_to_all(jnp.stack([vir_rows[0]] * lax.axis_size("band")), "band", 0, 0), axis=0
+        ),
     )
     auxiliary = vir_full.shape[0]
     occ_own = occ_rows[0]

time: 216 us -> 233 us (1.079)
  blocking collectives: 31.1 us -> 66.2 us
  waiting for transfers between devices: 82.9 us -> 68.5 us
  between operations: 13.5 us -> 0.16 us
  starting transfers between devices: 29.6 us -> 35.9 us
  local copies, waits for them, and re-layouts: 25 us -> 28.9 us
    all_gather x1, blocking collectives: 31.1 us -> 66.2 us  [per_device(): lax.all_gather(trial_half, 'band', axis=2, tiled=True)]
    all_gather x1 -> x0, waiting for transfers between devices: 13.7 us -> none  [per_device(): lax.all_gather(vir_rows[0], 'band', axis=0, tiled=True)]
    all_to_all x0 -> x1, starting transfers between devices: none -> 5.53 us  [per_device(): lax.all_to_all(jnp.stack([vir_rows[0]] * lax.axis_size('band')), 'band',...]
    another operation x0 -> x1, local copies, waits for them, and re-layouts: none -> 3.38 us  [per_device(): jnp.stack([vir_rows[0]] * lax.axis_size('band'))]
  transfers between devices with their start and end apart: 6 -> 6, of which waited for: 4 -> 3; matrix products, arithmetic and copies ran while one was open for 22% -> 20% of each run, Pallas kernels for 0% -> 0%
where the time goes in v1:
time: 233 us; the launch traced here: 232 us
  waiting for transfers between devices  68.5 us (29%)
  blocking collectives  66.2 us (28%)
  starting transfers between devices  35.9 us (15%)
  local copies, waits for them, and re-layouts  28.9 us (12%)
  other arithmetic  21.5 us (9%)
  matrix products  10.8 us (5%)
    all_gather x1, blocking collectives, per_device(): lax.all_gather(trial_half, 'band', axis=2, tiled=True)  66.2 us
    all_to_all x1, waiting for transfers between devices, per_device(): lax.all_to_all(summed.astype(jnp.bfloat16), 'ka', split_axis=2, concat_ax...  28.5 us
    all_to_all x1, waiting for transfers between devices, per_device(): lax.all_to_all(split_pairs, 'ka', split_axis=2, concat_axis=2, tiled=True)  26.1 us
    unnamed x2, other arithmetic  20.6 us
    gather x1, local copies, waits for them, and re-layouts, per_device(): jnp.take(lax.all_to_all(split_pairs, 'ka', split_axis=2, concat_axis=2, t...  13.9 us
    all_to_all x1, waiting for transfers between devices, summed_on_arrival(): pieces = lax.all_to_all(split_up(array, dim, size), axis, 0, 0, tiled=True)  13.9 us
    all_to_all x2, starting transfers between devices, sent_to_all(): return lax.all_to_all(copies, axis, split_axis=0, concat_axis=0, tiled=True)  10.4 us
    all_to_all x1, starting transfers between devices, per_device(): lax.all_to_all(split_pairs, 'ka', split_axis=2, concat_axis=2, tiled=True)  7.36 us
  transfers between devices with their start and end apart: 6, of which 3 were waited for; matrix products, arithmetic and copies ran while one was open for 20% of the time, Pallas kernels for 0%

profile of v1, /device:TPU:96, one launch (start us, length us, event | category | flops | bytes accessed | tf_op | source)
XLA Modules:
  0.0 231.9 jit_solution(280376242592551616)
XLA Ops:
  0.0 0.0 copy-start
  0.0 3.4 %stack.3 = bf16[8,256,896]{2,1,0:T(8,128)(2,1)} broadcast(bf16[256,896]{1,0:T(8,128)(2,1)} %bitcast.59), dimensions={1,2} | broadcast | bytes 4128768 | tf_op jit(solution)/shard_map/stack | solution.py:49
  3.4 0.0 copy-start.3
  3.4 5.5 %all-to-all-start.2 = ((bf16[8,256,896]{2,1,0:T(8,128)(2,1)}), bf16[8,256,896]{2,1,0:T(8,128)(2,1)}, u32[]{:S(2)}, u32[]{:S(2)}) async-start(bf16[8,256,896]{2,1,0:T(8,128)(2,1)} %stack.3), calls=%async_computation.2 | async-start | bytes 7340032 | tf_op jit(solution)/shard_map/all_to_all | solution.py:49
  8.9 0.0 copy-done.3
  8.9 0.0 copy-start.4
  8.9 0.0 copy-start.5
  8.9 0.1 bitcast_convert_fusion.1
  9.0 0.3 copy.30
  9.3 0.5 copy-done.4
  9.8 0.0 copy-start.2
  9.8 66.2 %all-gather = bf16[1,2,128,896]{2,3,1,0:T(8,128)(2,1)S(1)} all-gather(bf16[1,2,128,112]{2,3,1,0:T(8,128)(2,1)S(1)} %convert_element_type.33), channel_id=2, replica_groups=mesh['ka'=16,'band'=8] {'band'}, dimensions={3}, use_global_device_ids=true | all-gather | bytes 516096 | tf_op jit(solution)/shard_map/all_gather | solution.py:47
  76.1 0.0 copy-done.5
  76.1 0.4 multiply_reduce_fusion.1
  76.5 0.0 all-to-all-done.2
  76.5 0.6 broadcast_in_dim.23
  77.1 6.7 %all-to-all-start = ((f32[16,2,256]{2,1,0:T(2,128)}), f32[16,2,256]{2,1,0:T(2,128)S(1)}, u32[]{:S(2)}, u32[]{:S(2)}) async-start(f32[16,2,256]{2,1,0:T(2,128)} %broadcast_in_dim.23), calls=%async_computation | async-start | bytes 65536 | tf_op jit(solution)/shard_map/all_to_all | solution.py:9
  83.8 4.4 %fusion = bf16[2,32,16,8,128]{4,3,2,1,0:T(8,128)(2,1)S(1)} fusion(bf16[2,256,896]{1,2,0:T(8,128)(2,1)S(1)} %get-tuple-element.6, bf16[2048,896,1]{1,0,2:T(8,128)(2,1)} %bitcast.12), kind=kOutput, calls=%fused_computation.7 | convolution fusion | flops 1880096768 | bytes 6684672 | tf_op jit(solution)/shard_map/vra,na->vrn/dot_general | solution.py:58
  88.2 0.0 copy-done.2
  88.2 1.9 copy.55
  90.1 0.0 all-to-all-done
  90.2 0.0 copy-start.6
  90.2 7.4 %all-to-all-start.3 = ((bf16[2,256,16,128]{3,1,0,2:T(8,128)(2,1)}), bf16[2,256,16,128]{3,1,0,2:T(8,128)(2,1)S(1)}, u32[]{:S(2)}, u32[]{:S(2)}) async-start(bf16[2,256,16,128]{3,1,0,2:T(8,128)(2,1)} %bitcast.56), calls=%async_computation.3 | async-start | bytes 4194304 | tf_op jit(solution)/shard_map/all_to_all | solution.py:71
  97.5 0.0 copy-done.6
  97.5 0.1 reshape.62
  97.6 2.7 %bitcast_convert_fusion = f32[256,128,16]{1,0,2:T(8,128)} fusion(bf16[16,256,2048]{2,1,0:T(8,128)(2,1)} %param.14, s32[]{:T(128)S(6)} %select_n.12), kind=kLoop, calls=%fused_computation.12 | loop fusion | flops 524288 | bytes 3145732
  100.4 26.1 %all-to-all-done.3 = bf16[2,256,16,128]{3,1,0,2:T(8,128)(2,1)S(1)} async-done(((bf16[2,256,16,128]{3,1,0,2:T(8,128)(2,1)}), bf16[2,256,16,128]{3,1,0,2:T(8,128)(2,1)S(1)}, u32[]{:S(2)}, u32[]{:S(2)}) %all-to-all-start.3) | async-done | bytes 2097184 | tf_op jit(solution)/shard_map/all_to_all | solution.py:71
  126.4 0.0 copy-start.1
  126.4 0.6 broadcast_in_dim.24
  127.1 0.7 copy-done.1
  127.8 3.7 %all-to-all-start.1 = ((bf16[8,2,256]{2,1,0:T(2,128)(2,1)}), bf16[8,2,256]{2,1,0:T(2,128)(2,1)S(1)}, u32[]{:S(2)}, u32[]{:S(2)}) async-start(bf16[8,2,256]{2,1,0:T(2,128)(2,1)} %broadcast_in_dim.24), calls=%async_computation.1 | async-start | bytes 16384 | tf_op jit(solution)/shard_map/all_to_all | solution.py:9
  131.5 1.7 copy.34
  133.2 13.9 %gather_fusion = bf16[256,2,256,128]{3,2,1,0:T(8,128)(2,1)} fusion(bf16[2,256,16,128]{3,1,2,0:T(8,128)(2,1)S(1)} %copy.34, s32[1024]{0:T(1024)S(1)} %pad_clamp_fusion), kind=kCustom, calls=%fused_computation | custom fusion | bytes 67109888 | tf_op jit(solution)/shard_map/jit(_take)/gather | solution.py:70
  147.1 17.9 %multiply_reduce_fusion = bf16[256,128,2,16]{1,0,2,3:T(8,128)(2,1)S(1)} fusion(f32[256,128,16]{1,0,2:T(8,128)} %bitcast_convert_fusion, bf16[16,16,2,256,128]{4,3,2,1,0:T(8,128)(2,1)} %bitcast.55, pred[16,16]{1,0:T(8,128)(4,1)S(1)} %compare_and_fusion), kind=kLoop, calls=%fused_computation.1 | loop fusion | flops 66060288 | bytes 37748992
  165.0 2.6 %copy.47 = bf16[256,128,2,16]{0,1,2,3:T(8,128)(2,1)} copy(bf16[256,128,2,16]{1,0,2,3:T(8,128)(2,1)S(1)} %multiply_reduce_fusion) | data formatting | bytes 4194304 | tf_op jit(solution)/shard_map/vrkqc,qrc->vrkc/dot_general | solution.py:75
  167.6 0.0 all-to-all-done.1
  167.6 6.0 %all-to-all-start.4 = ((bf16[2,256,16,128]{1,3,0,2:T(8,128)(2,1)}), bf16[2,256,16,128]{1,3,0,2:T(8,128)(2,1)S(1)}, u32[]{:S(2)}, u32[]{:S(2)}) async-start(bf16[2,256,16,128]{1,3,0,2:T(8,128)(2,1)} %bitcast.57), calls=%async_computation.4 | async-start | bytes 4194304 | tf_op jit(solution)/shard_map/all_to_all | solution.py:78
  173.6 0.0 copy-done
  173.6 0.4 convolution_multiply_fusion
  174.0 28.5 %all-to-all-done.4 = bf16[2,256,16,128]{1,3,0,2:T(8,128)(2,1)S(1)} async-done(((bf16[2,256,16,128]{1,3,0,2:T(8,128)(2,1)}), bf16[2,256,16,128]{1,3,0,2:T(8,128)(2,1)S(1)}, u32[]{:S(2)}, u32[]{:S(2)}) %all-to-all-start.4) | async-done | bytes 2097184 | tf_op jit(solution)/shard_map/all_to_all | solution.py:78
  202.5 1.5 copy.35
  204.0 5.6 %fusion.2 = f32[2,896,128]{2,1,0:T(8,128)S(1)} fusion(bf16[2,256,2048]{1,2,0:T(8,128)(2,1)} %bitcast.58, bf16[2048,896,1]{1,0,2:T(8,128)(2,1)} %bitcast.12, f32[2,256]{1,0:T(2,128)S(1)} %convolution_multiply_fusion, f32[256,896]{0,1:T(8,128)} %copy-done.2, bf16[1,256,128]{2,1,0:T(8,128)(2,1)S(1)} %copy-done.5), kind=kOutput, calls=%fused_computation.10 | convolution fusion | flops 1997864960 | bytes 7669760 | tf_op jit(solution)/shard_map/ri,vra->via/dot_general | solution.py:86
  209.6 0.0 copy-start.7
  209.6 0.0 copy-start.8
  209.6 1.0 copy.56
  210.6 6.6 %all-to-all-start.5 = ((f32[8,2,128,112]{2,3,1,0:T(8,128)}), f32[8,2,128,112]{2,3,1,0:T(8,128)S(1)}, u32[]{:S(2)}, u32[]{:S(2)}) async-start(f32[8,2,128,112]{2,3,1,0:T(8,128)} %bitcast.54), calls=%async_computation.5 | async-start | bytes 1835008 | tf_op jit(solution)/shard_map/all_to_all | solution.py:34
  217.2 0.0 copy-done.7
  217.2 0.0 copy-done.8
  217.2 0.1 broadcast_subtract_fusion
  217.3 13.9 %all-to-all-done.5 = f32[8,2,128,112]{2,3,1,0:T(8,128)S(1)} async-done(((f32[8,2,128,112]{2,3,1,0:T(8,128)}), f32[8,2,128,112]{2,3,1,0:T(8,128)S(1)}, u32[]{:S(2)}, u32[]{:S(2)}) %all-to-all-start.5) | async-done | bytes 917536 | tf_op jit(solution)/shard_map/all_to_all | solution.py:34
  231.2 0.7 bitcast_add_fusion
  (6 shorter events, 0.1 us)
Async XLA Ops:
  0.0 173.6 %copy-start = (bf16[256,2048]{1,0:T(8,128)(2,1)S(1)}, bf16[256,2048]{1,0:T(8,128)(2,1)}, u32[]{:S(2)}) copy-start(bf16[256,2048]{1,0:T(8,128)(2,1)} %param.13) | copy-start | bytes 3145732
  3.4 5.5 %copy-start.3 = (bf16[1,256,896]{2,1,0:T(8,128)(2,1)S(1)}, bf16[1,256,896]{2,1,0:T(8,128)(2,1)}, u32[]{:S(2)}) copy-start(bf16[1,256,896]{2,1,0:T(8,128)(2,1)} %param.9) | copy-start | bytes 1376260
  3.4 73.1 %all-to-all-start.2 = ((bf16[8,256,896]{2,1,0:T(8,128)(2,1)}), bf16[8,256,896]{2,1,0:T(8,128)(2,1)}, u32[]{:S(2)}, u32[]{:S(2)}) async-start(bf16[8,256,896]{2,1,0:T(8,128)(2,1)} %stack.3), calls=%async_computation.2 | async-start | bytes 7340032 | tf_op jit(solution)/shard_map/all_to_all | solution.py:49
  8.9 0.9 copy-start.4
  8.9 67.1 %copy-start.5 = (bf16[1,256,128]{2,1,0:T(8,128)(2,1)S(1)}, bf16[1,256,128]{2,1,0:T(8,128)(2,1)}, u32[]{:S(2)}) copy-start(bf16[1,256,128]{2,1,0:T(8,128)(2,1)} %param.8) | copy-start | bytes 196612
  9.8 78.4 %copy-start.2 = (f32[256,896]{0,1:T(8,128)}, f32[256,896]{0,1:T(8,128)S(1)}, u32[]{:S(2)}) copy-start(f32[256,896]{0,1:T(8,128)S(1)} %copy.30) | copy-start | bytes 2752516
  77.1 13.0 %all-to-all-start = ((f32[16,2,256]{2,1,0:T(2,128)}), f32[16,2,256]{2,1,0:T(2,128)S(1)}, u32[]{:S(2)}, u32[]{:S(2)}) async-start(f32[16,2,256]{2,1,0:T(2,128)} %broadcast_in_dim.23), calls=%async_computation | async-start | bytes 65536 | tf_op jit(solution)/shard_map/all_to_all | solution.py:9
  90.2 7.4 %copy-start.6 = (s32[16,16]{1,0:T(8,128)S(1)}, s32[16,16]{1,0:T(8,128)}, u32[]{:S(2)}) copy-start(s32[16,16]{1,0:T(8,128)} %param.15) | copy-start | bytes 3076
  90.2 36.3 %all-to-all-start.3 = ((bf16[2,256,16,128]{3,1,0,2:T(8,128)(2,1)}), bf16[2,256,16,128]{3,1,0,2:T(8,128)(2,1)S(1)}, u32[]{:S(2)}, u32[]{:S(2)}) async-start(bf16[2,256,16,128]{3,1,0,2:T(8,128)(2,1)} %bitcast.56), calls=%async_computation.3 | async-start | bytes 4194304 | tf_op jit(solution)/shard_map/all_to_all | solution.py:71
  126.4 1.3 copy-start.1
  127.8 39.9 %all-to-all-start.1 = ((bf16[8,2,256]{2,1,0:T(2,128)(2,1)}), bf16[8,2,256]{2,1,0:T(2,128)(2,1)S(1)}, u32[]{:S(2)}, u32[]{:S(2)}) async-start(bf16[8,2,256]{2,1,0:T(2,128)(2,1)} %broadcast_in_dim.24), calls=%async_computation.1 | async-start | bytes 16384 | tf_op jit(solution)/shard_map/all_to_all | solution.py:9
  167.6 34.9 %all-to-all-start.4 = ((bf16[2,256,16,128]{1,3,0,2:T(8,128)(2,1)}), bf16[2,256,16,128]{1,3,0,2:T(8,128)(2,1)S(1)}, u32[]{:S(2)}, u32[]{:S(2)}) async-start(bf16[2,256,16,128]{1,3,0,2:T(8,128)(2,1)} %bitcast.57), calls=%async_computation.4 | async-start | bytes 4194304 | tf_op jit(solution)/shard_map/all_to_all | solution.py:78
  209.6 7.6 %copy-start.7 = (f32[1,128]{1,0:T(1,128)S(1)}, f32[1,128]{1,0:T(1,128)}, u32[]{:S(2)}) copy-start(f32[1,128]{1,0:T(1,128)} %param.11) | copy-start | bytes 1540
  209.6 7.6 %copy-start.8 = (f32[1,112]{1,0:T(1,128)S(1)}, f32[1,112]{1,0:T(1,128)}, u32[]{:S(2)}) copy-start(f32[1,112]{1,0:T(1,128)} %param.12) | copy-start | bytes 1348
  210.6 20.6 %all-to-all-start.5 = ((f32[8,2,128,112]{2,3,1,0:T(8,128)}), f32[8,2,128,112]{2,3,1,0:T(8,128)S(1)}, u32[]{:S(2)}, u32[]{:S(2)}) async-start(f32[8,2,128,112]{2,3,1,0:T(8,128)} %bitcast.54), calls=%async_computation.5 | async-start | bytes 1835008 | tf_op jit(solution)/shard_map/all_to_all | solution.py:34
